TPU v7x, 512 devices: a 4x2x32 block of a 4x8x32 slice. The times are simulated.
512 devices in a mesh: groups: 2 (over y), dp: 4 (over x), tensor: 64 (over z, core).
Axes of the slice: x: 4, y: 2, z: 32, core: 2. Of those that a mesh axis runs over, the one named last changes fastest.
The devices are a block of a 4x8x32 slice.
Arguments:
- tokens: bfloat16 [1024, 8192], P(('groups', 'dp'), 'tensor'), parts along dimension 0, may hold values from -6 to 6
- gate_up_weight: bfloat16 [8192, 32768], P('dp', 'tensor'), may hold values from -0.0625 to 0.0625
- down_weight: bfloat16 [16384, 8192], P('tensor', 'dp'), may hold values from -0.046875 to 0.046875
Outputs:
- mixed_out: bfloat16 [1024, 8192], P(('groups', 'dp'), 'tensor'), parts along dimension 0
There are 2 independent parts, one for each index of `groups`. A program takes and returns all parts, laid end to end along the dimension named above; an argument that names none is the same for every part. Nothing has to cross between parts.
All inputs are finite; a program needn't handle non-finite values.
Results may differ from a plain program's by a relative error of at most 0.0049.
Values may be sent and summed in bfloat16 or wider, within the bound.
No kernel may reach another device: no remote copies, remote signals or barrier semaphores. Data moves between devices by JAX's collectives and lax.ppermute only.
A program may use at most 64 MiB of HBM per device.

v0:
```python
import jax
import jax.numpy as jnp
from jax import lax
from jax.experimental import pallas as pl
from jax.experimental.pallas import tpu as pltpu
from jax.sharding import Mesh
from jax.sharding import PartitionSpec as P


Z = ("zo", "zi")
TENSOR = ("zo", "zi", "core")
F32 = jnp.float32
BF16 = jnp.bfloat16

STEPS = (1, 2, 3, 4)


def shifted(array, by, cores=(0, 1)):
    n = lax.axis_size(Z)
    pairs = [(2 * i + c, 2 * ((i + (by, -by)[c]) % n) + c) for i in range(n) for c in cores]
    return lax.ppermute(array, TENSOR, pairs)


def residue_at(step, core):
    n = lax.axis_size("zi")
    return lax.rem(lax.axis_index("zi") + jnp.where(core == 0, n - step, step), n)


def whole(start, size):
    return pl.ds(pl.multiple_of(start, size), size)


def swapped(array):
    return lax.ppermute(array, "core", [(0, 1), (1, 0)])


def vmem_call(kernel, outs, *args, flops, scratch=()):
    vmem = pl.BlockSpec(memory_space=pltpu.VMEM)
    flat, tree = jax.tree.flatten(args)
    size = sum(a.size * a.dtype.itemsize for a in (*flat, *jax.tree.leaves(outs)))

    def body(*refs):
        kernel(*jax.tree.unflatten(tree, refs[: len(flat)]), *refs[len(flat) :])

    return pl.pallas_call(
        body,
        out_shape=outs,
        in_specs=[vmem] * len(flat),
        out_specs=jax.tree.map(lambda _: vmem, outs),
        scratch_shapes=scratch,
        compiler_params=pltpu.CompilerParams(vmem_limit_bytes=40 * 2**20),
        cost_estimate=pl.CostEstimate(flops=flops, bytes_accessed=size, transcendentals=0),
    )(*flat)


def add_product(total, ref, at, half, weight_ref, residue):
    blocks = range(at, at + lax.axis_size("dp"), 2)
    data = jnp.concatenate([jnp.concatenate([ref[k], ref[k + 1]], axis=1) for k in blocks])
    rows, width = data.shape
    weight = weight_ref[whole(residue * width, width), :]
    total[whole(half * rows, rows), :] += jnp.dot(data, weight, preferred_element_type=F32)


def near_kernel(own_ref, one_ref, two_refs, three_ref, four_refs, weight_ref, total):
    core, n = lax.axis_index("core"), lax.axis_size("dp")
    total[...] = jnp.zeros_like(total)
    for half in (0, 1):
        add_product(total, own_ref, half * n, half, weight_ref, lax.axis_index("zi"))
        add_product(total, one_ref, half * n, half, weight_ref, residue_at(1, core))
        add_product(total, two_refs[half], 0, half, weight_ref, residue_at(2, core))
        add_product(total, three_ref, half * n, half, weight_ref, residue_at(3, core))
        add_product(total, four_refs[half], 0, half, weight_ref, residue_at(4, core))


def up_kernel(total_in_ref, theirs_ref, weight_ref, out_ref, rest_ref, total):
    core, n = lax.axis_index("core"), lax.axis_size("dp")
    total[...] = total_in_ref[...]
    for k in range(8):
        add_product(total, theirs_ref, k * n, k % 2, weight_ref, residue_at(k // 2 + 1, 1 - core))
    columns = total.shape[1]
    row = lax.broadcasted_iota(jnp.int32, (columns, columns), 0)
    col = lax.broadcasted_iota(jnp.int32, (columns, columns), 1)
    half = columns // 2
    pick = (row == jnp.where(col < half, 2 * col, 2 * (col - half) + 1)).astype(BF16)
    out_ref[...] = jnp.dot(total[...].astype(BF16), pick, preferred_element_type=F32).astype(BF16)
    rows = rest_ref.shape[0]
    stay = total[whole(lax.axis_index("dp") * rows, rows), :]
    rest = (stay - stay.astype(BF16).astype(F32)).astype(BF16)
    rest_ref[...] = jnp.dot(rest, pick, preferred_element_type=F32).astype(BF16)


def hidden_kernel(parts_ref, rest_ref, out_ref):
    total = parts_ref[0].astype(F32) + rest_ref[...].astype(F32)
    for k in range(1, parts_ref.shape[0]):
        total += parts_ref[k].astype(F32)
    half = total.shape[1] // 2
    gate, up = total[:, :half], total[:, half:]
    out_ref[...] = (gate / (1.0 + jnp.exp(-gate)) * up).astype(BF16)


def down_kernel(hidden_ref, weight_ref, other_weight_ref, four_ref, three_ref, one_ref, two_ref, own_ref):
    core = lax.axis_index("core")
    mine, theirs = hidden_ref.at[core], hidden_ref.at[1 - core]

    def term(start, width):
        cols = pl.ds(pl.multiple_of(start, 128), width)
        out = jnp.dot(mine[...], weight_ref[:, cols], preferred_element_type=F32)
        return out + jnp.dot(theirs[...], other_weight_ref[:, cols], preferred_element_type=F32)

    width = four_ref.shape[1]
    for step, ref in zip(STEPS, (one_ref, two_ref, three_ref, four_ref)):
        ref[...] = term(residue_at(step, core) * width, width).astype(ref.dtype)
    half = own_ref.shape[1]
    own_ref[...] = term(lax.axis_index("zi") * width + core * half, half)


def give_kernel(one_ref, two_ref, out_ref):
    width = out_ref.shape[1]
    cols = whole((1 - lax.axis_index("core")) * width, width)
    out_ref[...] = one_ref[:, cols].astype(F32) + two_ref[:, cols].astype(F32)


def window_kernel(own_ref, one_ref, two_ref, given_ref, out_ref):
    core = lax.axis_index("core")
    width = own_ref.shape[1]
    cols = whole(core * width, width)
    total = own_ref[...] + one_ref[:, cols].astype(F32) + two_ref[:, cols].astype(F32)
    out_ref[...] = (total + given_ref[1 - core]).astype(BF16)


def per_device(tokens, gate_up_weight, down_weight):
    rows, width = tokens.shape
    columns = gate_up_weight.shape[1]
    dp = lax.axis_size("dp")
    shape = jax.ShapeDtypeStruct
    other_weight = swapped(down_weight)
    copies = lax.all_gather(tokens, "zo", axis=0)
    copies = jnp.repeat(copies, 2, axis=0)
    pair = lax.all_to_all(copies, ("dp", "core"), split_axis=0, concat_axis=0, tiled=True)
    halves = (pair[:dp], pair[dp:])
    halves, pair = lax.optimization_barrier((halves, pair))
    first = shifted(halves[0], 2)
    second = shifted(halves[1], 2)
    one = shifted(pair, 1)
    first, other_weight = lax.optimization_barrier((first, other_weight))
    two = (first, second)
    four = tuple(shifted(a, 2, cores=(1,)) for a in two)
    three = shifted(jnp.concatenate(two), 1)
    theirs = swapped(jnp.concatenate([one, *two, three, *four]))
    total = vmem_call(
        near_kernel,
        shape((dp * rows, columns), F32),
        pair,
        one,
        two,
        three,
        four,
        gate_up_weight,
        flops=dp * rows * gate_up_weight.size,
    )
    partial_value, rest = vmem_call(
        up_kernel,
        (shape((dp * rows, columns), BF16), shape((rows, columns), BF16)),
        total,
        theirs,
        gate_up_weight,
        flops=dp * rows * gate_up_weight.size,
        scratch=[pltpu.VMEM((dp * rows, columns), F32)],
    )
    parts = partial_value.reshape(dp, rows, columns)
    parts = lax.all_to_all(parts, "dp", split_axis=0, concat_axis=0, tiled=True)
    own_hidden = vmem_call(
        hidden_kernel, shape((rows, columns // 2), BF16), parts, rest, flops=10 * parts.size
    )
    hidden = jnp.broadcast_to(own_hidden[None], (dp, *own_hidden.shape))
    hidden = lax.all_to_all(hidden, "dp", split_axis=0, concat_axis=0, tiled=True)
    hidden = lax.all_gather(hidden.reshape(dp * rows, columns // 2), "core", axis=0)

    block = (dp * rows, 2 * width)
    four, three, one, two, own = vmem_call(
        down_kernel,
        (shape(block, BF16),) * 3 + (shape(block, F32), shape((dp * rows, width), F32)),
        hidden,
        down_weight,
        other_weight,
        flops=4 * dp * rows * down_weight.size,
    )
    four = shifted(four, -2, cores=(1,))
    three = shifted(three, -1)
    one = shifted(one, -1)
    two = shifted((two + three.astype(F32) + four.astype(F32)).astype(BF16), -2)
    given = vmem_call(give_kernel, shape((dp * rows, width), F32), one, two, flops=2 * own.size)
    given = lax.all_gather(given, "core", axis=0)
    out = vmem_call(window_kernel, shape((dp * rows, width), BF16), own, one, two, given, flops=4 * own.size)
    out = out.reshape(dp, rows, width)
    out = lax.all_to_all(out, "dp", split_axis=0, concat_axis=0, tiled=True)
    out = lax.all_to_all(out, "zo", split_axis=0, concat_axis=0, tiled=True)
    return out.astype(F32).sum(axis=0).astype(BF16)


def solution(mesh):
    dp, tensor = mesh.shape["dp"], mesh.shape["tensor"]
    split = Mesh(
        mesh.devices.reshape(mesh.shape["groups"], dp, dp, tensor // (2 * dp), 2),
        ("groups", "dp", *TENSOR),
    )
    placed = (P(("groups", "dp"), TENSOR), P("dp", TENSOR), P(TENSOR, "dp"))
    return jax.shard_map(
        per_device,
        mesh=split,
        in_specs=placed,
        out_specs=P(("groups", "dp"), TENSOR),
        check_vma=False,
    )
```

profile of v0, /device:TPU:96, one launch (start us, length us, event | category | flops | bytes accessed | tf_op | source)
XLA Modules:
  0.0 218.2 jit_solution(17790813323012752953)
XLA Ops:
  0.0 0.0 copy-start
  0.0 2.1 collective-permute-start.2
  2.1 61.9 %all-gather = bf16[512,128]{1,0:T(8,128)(2,1)S(1)} all-gather(bf16[128,128]{1,0:T(8,128)(2,1)} %param.3), channel_id=2, replica_groups=mesh['groups'=2,'dp'=4,'zo'=4,'zi'=8,'core'=2] {'zo'}, dimensions={0}, use_global_device_ids=true | all-gather | bytes 163840 | tf_op jit(solution)/shard_map/all_gather | solution.py:137
  64.0 11.5 %all_to_all.25.refs_0_ = bf16[8,128,128]{2,1,0:T(8,128)(2,1)S(1)} all-to-all(bf16[8,128,128]{2,1,0:T(8,128)(2,1)S(1)} %bitcast.10), channel_id=1, replica_groups=mesh['groups'=2,'dp'=4,'zo'=4,'zi'=8,'core'=2] {'dp','core'}, dimensions={0} | all-to-all | bytes 524288 | tf_op jit(solution)/shard_map/all_to_all | solution.py:139
  75.5 4.0 %collective-permute-start = (bf16[8,128,128]{2,1,0:T(8,128)(2,1)S(1)}, bf16[8,128,128]{2,1,0:T(8,128)(2,1)S(1)}, u32[]{:S(2)}, u32[]{:S(2)}) collective-permute-start(bf16[8,128,128]{2,1,0:T(8,128)(2,1)S(1)} %all_to_all.25.refs_0_), channel_id=1, source_target_pairs={{0,2},{1,63},{2,4},{3,1},{4,6},{5,3},{6,8},{7,5},{8,10},{9,7},{10,... | collective-permute-start | bytes 786440 | tf_op jit(solution)/shard_map/ppermute | solution.py:21
  79.5 5.1 %collective-permute-start.3 = (bf16[4,128,128]{2,1,0:T(8,128)(2,1)S(1)}, bf16[4,128,128]{2,1,0:T(8,128)(2,1)S(1)}, u32[]{:S(2)}, u32[]{:S(2)}) collective-permute-start(bf16[4,128,128]{2,1,0:T(8,128)(2,1)S(1)} %get-tuple-element.20), channel_id=1, source_target_pairs={{0,4},{1,61},{2,6},{3,63},{4,8},{5,1},{6,10},{7,3},{8,12},{9,5},{1... | collective-permute-start | bytes 393224 | tf_op jit(solution)/shard_map/ppermute | solution.py:21
  84.6 6.2 %collective-permute-start.1 = (bf16[4,128,128]{2,1,0:T(8,128)(2,1)S(1)}, bf16[4,128,128]{2,1,0:T(8,128)(2,1)S(1)}, u32[]{:S(2)}, u32[]{:S(2)}) collective-permute-start(bf16[4,128,128]{2,1,0:T(8,128)(2,1)S(1)} %get-tuple-element.18), channel_id=1, source_target_pairs={{0,4},{1,61},{2,6},{3,63},{4,8},{5,1},{6,10},{7,3},{8,12},{9,5},{1... | collective-permute-start | bytes 393224 | tf_op jit(solution)/shard_map/ppermute | solution.py:21
  90.8 5.9 %collective-permute-done.3.refs_3_ = bf16[4,128,128]{2,1,0:T(8,128)(2,1)S(1)} collective-permute-done((bf16[4,128,128]{2,1,0:T(8,128)(2,1)S(1)}, bf16[4,128,128]{2,1,0:T(8,128)(2,1)S(1)}, u32[]{:S(2)}, u32[]{:S(2)}) %collective-permute-start.3) | collective-permute-done | bytes 131104 | tf_op jit(solution)/shard_map/ppermute | solution.py:21
  96.8 0.7 collective-permute-start.6
  97.4 0.9 collective-permute-done.1.refs_2_
  98.3 0.0 collective-permute-done.2.refs_2_
  98.3 2.0 collective-permute-start.4
  100.3 0.0 collective-permute-done.refs_1_
  100.3 0.7 collective-permute-start.5
  101.1 8.2 %collective-permute-done.4.refs_4_ = bf16[8,128,128]{2,1,0:T(8,128)(2,1)S(1)} collective-permute-done((bf16[8,128,128]{2,1,0:T(8,128)(2,1)S(1)}, bf16[8,128,128]{2,1,0:T(8,128)(2,1)S(1)}, u32[]{:S(2)}, u32[]{:S(2)}) %collective-permute-start.4) | collective-permute-done | bytes 262176 | tf_op jit(solution)/shard_map/ppermute | solution.py:21
  109.3 0.0 collective-permute-done.5.refs_5_
  109.4 0.0 collective-permute-done.6.refs_6_
  109.4 3.7 %collective-permute-start.7 = (bf16[32,128,128]{2,1,0:T(8,128)(2,1)S(1)}, bf16[32,128,128]{2,1,0:T(8,128)(2,1)S(1)}, u32[]{:S(2)}, u32[]{:S(2)}) collective-permute-start(bf16[32,128,128]{2,1,0:T(8,128)(2,1)S(1)} %constant_dynamic-update-slice_fusion), channel_id=1, source_target_pairs={{0,1},{1,0},{2,3},{3,2},{4,5},{5,4},{6,7},{7,6},{8,9},{9,8},{10,11... | collective-permute-start | bytes 3145736 | tf_op jit(solution)/shard_map/ppermute | solution.py:34
  113.2 0.0 copy-done
  113.2 0.8 shard_map.37.refs_0_
  114.0 1.4 collective-permute-done.7.refs_1_
  115.4 1.1 shard_map.38
  116.5 0.0 copy-start.1
  116.5 12.9 %all_to_all.26.refs_0_ = bf16[4,128,512]{2,1,0:T(8,128)(2,1)S(1)} all-to-all(bf16[4,128,512]{2,1,0:T(8,128)(2,1)S(1)} %bitcast.7), channel_id=1, replica_groups=mesh['groups'=2,'dp'=4,'zo'=4,'zi'=8,'core'=2] {'dp'}, dimensions={0} | all-to-all | bytes 1048576 | tf_op jit(solution)/shard_map/all_to_all | solution.py:171
  129.4 0.1 shard_map.39
  129.5 9.1 %all_to_all.27 = bf16[4,128,256]{2,1,0:T(8,128)(2,1)S(1)} all-to-all(bf16[4,128,256]{2,1,0:T(8,128)(2,1)S(1)} %broadcast_in_dim.10), channel_id=1, replica_groups=mesh['groups'=2,'dp'=4,'zo'=4,'zi'=8,'core'=2] {'dp'}, dimensions={0} | all-to-all | bytes 524288 | tf_op jit(solution)/shard_map/all_to_all | solution.py:176
  138.6 2.2 %all_gather.17.refs_0_ = bf16[2,512,256]{2,1,0:T(8,128)(2,1)S(1)} all-gather(bf16[1,512,256]{2,1,0:T(8,128)(2,1)S(1)} %bitcast.9), channel_id=1, replica_groups=mesh['groups'=2,'dp'=4,'zo'=4,'zi'=8,'core'=2] {'core'}, dimensions={0}, use_global_device_ids=true | all-gather | bytes 786432 | tf_op jit(solution)/shard_map/all_gather | solution.py:177
  140.8 0.0 copy-done.1
  140.8 0.9 shard_map.40
  141.7 3.8 %collective-permute-start.9 = (bf16[512,256]{1,0:T(8,128)(2,1)S(1)}, bf16[512,256]{1,0:T(8,128)(2,1)S(1)}, u32[]{:S(2)}, u32[]{:S(2)}) collective-permute-start(bf16[512,256]{1,0:T(8,128)(2,1)S(1)} %get-tuple-element.27), channel_id=1, source_target_pairs={{0,62},{1,3},{2,0},{3,5},{4,2},{5,7},{6,4},{7,9},{8,6},{9,11},{10,... | collective-permute-start | bytes 786440 | tf_op jit(solution)/shard_map/ppermute | solution.py:21
  145.5 0.7 collective-permute-start.10
  146.2 4.0 %collective-permute-start.8 = (bf16[512,256]{1,0:T(8,128)(2,1)S(1)}, bf16[512,256]{1,0:T(8,128)(2,1)S(1)}, u32[]{:S(2)}, u32[]{:S(2)}) collective-permute-start(bf16[512,256]{1,0:T(8,128)(2,1)S(1)} %get-tuple-element.25), channel_id=1, source_target_pairs={{0,62},{1,3},{2,0},{3,5},{4,2},{5,7},{6,4},{7,9},{8,6},{9,11},{10,... | collective-permute-start | bytes 786440 | tf_op jit(solution)/shard_map/ppermute | solution.py:21
  150.3 0.9 collective-permute-done.9
  151.1 0.0 collective-permute-done.10
  151.1 0.1 add_convert_fusion
  151.2 5.4 %collective-permute-start.11 = (bf16[512,256]{1,0:T(8,128)(2,1)S(1)}, bf16[512,256]{1,0:T(8,128)(2,1)S(1)}, u32[]{:S(2)}, u32[]{:S(2)}) collective-permute-start(bf16[512,256]{1,0:T(8,128)(2,1)S(1)} %add_convert_fusion), channel_id=1, source_target_pairs={{0,60},{1,5},{2,62},{3,7},{4,0},{5,9},{6,2},{7,11},{8,4},{9,13},{1... | collective-permute-start | bytes 786440 | tf_op jit(solution)/shard_map/ppermute | solution.py:21
  156.7 0.0 collective-permute-done.8.refs_0_.refs_1_
  156.7 5.9 %collective-permute-done.11.refs_1_.refs_2_ = bf16[512,256]{1,0:T(8,128)(2,1)S(1)} collective-permute-done((bf16[512,256]{1,0:T(8,128)(2,1)S(1)}, bf16[512,256]{1,0:T(8,128)(2,1)S(1)}, u32[]{:S(2)}, u32[]{:S(2)}) %collective-permute-start.11) | collective-permute-done | bytes 262176 | tf_op jit(solution)/shard_map/ppermute | solution.py:21
  162.6 6.6 %all-gather.1 = f32[1024,128]{1,0:T(8,128)S(1)} all-gather(f32[512,128]{1,0:T(8,128)S(1)} %shard_map.41), channel_id=3, replica_groups=mesh['groups'=2,'dp'=4,'zo'=4,'zi'=8,'core'=2] {'core'}, dimensions={0}, use_global_device_ids=true | all-gather | bytes 786432 | tf_op jit(solution)/shard_map/all_gather | solution.py:193
  169.2 0.1 shard_map.42
  169.2 8.5 %all_to_all.28 = bf16[4,128,128]{2,1,0:T(8,128)(2,1)S(1)} all-to-all(bf16[4,128,128]{2,1,0:T(8,128)(2,1)S(1)} %bitcast.8), channel_id=1, replica_groups=mesh['groups'=2,'dp'=4,'zo'=4,'zi'=8,'core'=2] {'dp'}, dimensions={0} | all-to-all | bytes 262144 | tf_op jit(solution)/shard_map/all_to_all | solution.py:196
  177.7 39.8 %all_to_all.29 = bf16[4,128,128]{2,1,0:T(8,128)(2,1)S(1)} all-to-all(bf16[4,128,128]{2,1,0:T(8,128)(2,1)S(1)} %all_to_all.28), channel_id=1, replica_groups=mesh['groups'=2,'dp'=4,'zo'=4,'zi'=8,'core'=2] {'zo'}, dimensions={0} | all-to-all | bytes 262144 | tf_op jit(solution)/shard_map/all_to_all | solution.py:197
  217.6 0.6 reduce_sum.12
  (11 shorter events, 0.3 us)
Async XLA Ops:
  0.0 113.2 %copy-start = (bf16[2048,512]{1,0:T(8,128)(2,1)S(1)}, bf16[2048,512]{1,0:T(8,128)(2,1)}, u32[]{:S(2)}) copy-start(bf16[2048,512]{1,0:T(8,128)(2,1)} %refs_2_.1) | copy-start | bytes 6291460
  0.0 98.3 %collective-permute-start.2 = (bf16[256,2048]{1,0:T(8,128)(2,1)}, bf16[256,2048]{1,0:T(8,128)(2,1)S(1)}, u32[]{:S(2)}, u32[]{:S(2)}) collective-permute-start(bf16[256,2048]{1,0:T(8,128)(2,1)} %refs_1_.1), channel_id=1, source_target_pairs={{0,1},{1,0},{2,3},{3,2},{4,5},{5,4},{6,7},{7,6},{8,9},{9,8},{10,11... | collective-permute-start | bytes 3145736 | tf_op jit(solution)/shard_map/ppermute | solution.py:34
  75.5 24.8 %collective-permute-start = (bf16[8,128,128]{2,1,0:T(8,128)(2,1)S(1)}, bf16[8,128,128]{2,1,0:T(8,128)(2,1)S(1)}, u32[]{:S(2)}, u32[]{:S(2)}) collective-permute-start(bf16[8,128,128]{2,1,0:T(8,128)(2,1)S(1)} %all_to_all.25.refs_0_), channel_id=1, source_target_pairs={{0,2},{1,63},{2,4},{3,1},{4,6},{5,3},{6,8},{7,5},{8,10},{9,7},{10,... | collective-permute-start | bytes 786440 | tf_op jit(solution)/shard_map/ppermute | solution.py:21
  79.5 17.3 %collective-permute-start.3 = (bf16[4,128,128]{2,1,0:T(8,128)(2,1)S(1)}, bf16[4,128,128]{2,1,0:T(8,128)(2,1)S(1)}, u32[]{:S(2)}, u32[]{:S(2)}) collective-permute-start(bf16[4,128,128]{2,1,0:T(8,128)(2,1)S(1)} %get-tuple-element.20), channel_id=1, source_target_pairs={{0,4},{1,61},{2,6},{3,63},{4,8},{5,1},{6,10},{7,3},{8,12},{9,5},{1... | collective-permute-start | bytes 393224 | tf_op jit(solution)/shard_map/ppermute | solution.py:21
  84.6 13.7 %collective-permute-start.1 = (bf16[4,128,128]{2,1,0:T(8,128)(2,1)S(1)}, bf16[4,128,128]{2,1,0:T(8,128)(2,1)S(1)}, u32[]{:S(2)}, u32[]{:S(2)}) collective-permute-start(bf16[4,128,128]{2,1,0:T(8,128)(2,1)S(1)} %get-tuple-element.18), channel_id=1, source_target_pairs={{0,4},{1,61},{2,6},{3,63},{4,8},{5,1},{6,10},{7,3},{8,12},{9,5},{1... | collective-permute-start | bytes 393224 | tf_op jit(solution)/shard_map/ppermute | solution.py:21
  96.8 12.6 %collective-permute-start.6 = (bf16[4,128,128]{2,1,0:T(8,128)(2,1)S(1)}, bf16[4,128,128]{2,1,0:T(8,128)(2,1)S(1)}, u32[]{:S(2)}, u32[]{:S(2)}) collective-permute-start(bf16[4,128,128]{2,1,0:T(8,128)(2,1)S(1)} %collective-permute-done.3.refs_3_), channel_id=1, source_target_pairs={{1,61},{3,63},{5,1},{7,3},{9,5},{11,7},{13,9},{15,11},{17,13},{19,... | collective-permute-start | bytes 393224 | tf_op jit(solution)/shard_map/ppermute | solution.py:21
  98.3 11.0 %collective-permute-start.4 = (bf16[8,128,128]{2,1,0:T(8,128)(2,1)S(1)}, bf16[8,128,128]{2,1,0:T(8,128)(2,1)S(1)}, u32[]{:S(2)}, u32[]{:S(2)}) collective-permute-start(bf16[8,128,128]{2,1,0:T(8,128)(2,1)S(1)} %pad_maximum_fusion), channel_id=1, source_target_pairs={{0,2},{1,63},{2,4},{3,1},{4,6},{5,3},{6,8},{7,5},{8,10},{9,7},{10,... | collective-permute-start | bytes 786440 | tf_op jit(solution)/shard_map/ppermute | solution.py:21
  100.3 9.0 %collective-permute-start.5 = (bf16[4,128,128]{2,1,0:T(8,128)(2,1)S(1)}, bf16[4,128,128]{2,1,0:T(8,128)(2,1)S(1)}, u32[]{:S(2)}, u32[]{:S(2)}) collective-permute-start(bf16[4,128,128]{2,1,0:T(8,128)(2,1)S(1)} %collective-permute-done.1.refs_2_), channel_id=1, source_target_pairs={{1,61},{3,63},{5,1},{7,3},{9,5},{11,7},{13,9},{15,11},{17,13},{19,... | collective-permute-start | bytes 393224 | tf_op jit(solution)/shard_map/ppermute | solution.py:21
  109.4 6.0 %collective-permute-start.7 = (bf16[32,128,128]{2,1,0:T(8,128)(2,1)S(1)}, bf16[32,128,128]{2,1,0:T(8,128)(2,1)S(1)}, u32[]{:S(2)}, u32[]{:S(2)}) collective-permute-start(bf16[32,128,128]{2,1,0:T(8,128)(2,1)S(1)} %constant_dynamic-update-slice_fusion), channel_id=1, source_target_pairs={{0,1},{1,0},{2,3},{3,2},{4,5},{5,4},{6,7},{7,6},{8,9},{9,8},{10,11... | collective-permute-start | bytes 3145736 | tf_op jit(solution)/shard_map/ppermute | solution.py:34
  116.5 24.3 %copy-start.1 = (bf16[256,2048]{1,0:T(8,128)(2,1)S(1)}, bf16[256,2048]{1,0:T(8,128)(2,1)}, u32[]{:S(2)}) copy-start(bf16[256,2048]{1,0:T(8,128)(2,1)} %refs_1_.1) | copy-start | bytes 3145732
  141.7 9.4 %collective-permute-start.9 = (bf16[512,256]{1,0:T(8,128)(2,1)S(1)}, bf16[512,256]{1,0:T(8,128)(2,1)S(1)}, u32[]{:S(2)}, u32[]{:S(2)}) collective-permute-start(bf16[512,256]{1,0:T(8,128)(2,1)S(1)} %get-tuple-element.27), channel_id=1, source_target_pairs={{0,62},{1,3},{2,0},{3,5},{4,2},{5,7},{6,4},{7,9},{8,6},{9,11},{10,... | collective-permute-start | bytes 786440 | tf_op jit(solution)/shard_map/ppermute | solution.py:21
  145.5 5.6 %collective-permute-start.10 = (bf16[512,256]{1,0:T(8,128)(2,1)S(1)}, bf16[512,256]{1,0:T(8,128)(2,1)S(1)}, u32[]{:S(2)}, u32[]{:S(2)}) collective-permute-start(bf16[512,256]{1,0:T(8,128)(2,1)S(1)} %get-tuple-element.28), channel_id=1, source_target_pairs={{1,5},{3,7},{5,9},{7,11},{9,13},{11,15},{13,17},{15,19},{17,21},{1... | collective-permute-start | bytes 786440 | tf_op jit(solution)/shard_map/ppermute | solution.py:21
  146.2 10.4 %collective-permute-start.8 = (bf16[512,256]{1,0:T(8,128)(2,1)S(1)}, bf16[512,256]{1,0:T(8,128)(2,1)S(1)}, u32[]{:S(2)}, u32[]{:S(2)}) collective-permute-start(bf16[512,256]{1,0:T(8,128)(2,1)S(1)} %get-tuple-element.25), channel_id=1, source_target_pairs={{0,62},{1,3},{2,0},{3,5},{4,2},{5,7},{6,4},{7,9},{8,6},{9,11},{10,... | collective-permute-start | bytes 786440 | tf_op jit(solution)/shard_map/ppermute | solution.py:21
  151.2 11.3 %collective-permute-start.11 = (bf16[512,256]{1,0:T(8,128)(2,1)S(1)}, bf16[512,256]{1,0:T(8,128)(2,1)S(1)}, u32[]{:S(2)}, u32[]{:S(2)}) collective-permute-start(bf16[512,256]{1,0:T(8,128)(2,1)S(1)} %add_convert_fusion), channel_id=1, source_target_pairs={{0,60},{1,5},{2,62},{3,7},{4,0},{5,9},{6,2},{7,11},{8,4},{9,13},{1... | collective-permute-start | bytes 786440 | tf_op jit(solution)/shard_map/ppermute | solution.py:21
where the time goes:
time: 219 us; the launch traced here: 218 us
  blocking collectives  152 us (69%)
  starting transfers between devices  38.3 us (17%)
  waiting for transfers between devices  23.2 us (11%)
  Pallas kernels  3 us (1%)
    all_gather x1, blocking collectives, per_device(): copies = lax.all_gather(tokens, 'zo', axis=0)  61.9 us
    all_to_all x1, blocking collectives, per_device(): out = lax.all_to_all(out, 'zo', split_axis=0, concat_axis=0, tiled=True)  39.8 us
    ppermute x10, starting transfers between devices, shifted(): return lax.ppermute(array, TENSOR, pairs)  32.5 us
    ppermute x10, waiting for transfers between devices, shifted(): return lax.ppermute(array, TENSOR, pairs)  21.8 us
    all_to_all x1, blocking collectives, per_device(): parts = lax.all_to_all(parts, 'dp', split_axis=0, concat_axis=0, tiled=True)  12.9 us
    all_to_all x1, blocking collectives, per_device(): lax.all_to_all(copies, ('dp', 'core'), split_axis=0, concat_axis=0, tiled...  11.5 us
    all_to_all x1, blocking collectives, per_device(): lax.all_to_all(hidden, 'dp', split_axis=0, concat_axis=0, tiled=True)  9.1 us
    all_to_all x1, blocking collectives, per_device(): out = lax.all_to_all(out, 'dp', split_axis=0, concat_axis=0, tiled=True)  8.5 us
  transfers between devices with their start and end apart: 12, of which 6 were waited for; matrix products, arithmetic and copies ran while one was open for 0% of the time, Pallas kernels for 0%

commit v1 on v0

--- a/solution.py
+++ b/solution.py
@@ -72,11 +72,12 @@
         add_product(total, four_refs[half], 0, half, weight_ref, residue_at(4, core))
 
 
-def up_kernel(total_in_ref, theirs_ref, weight_ref, out_ref, rest_ref, total):
+def up_kernel(total_in_ref, early_ref, late_ref, weight_ref, out_ref, rest_ref, total):
     core, n = lax.axis_index("core"), lax.axis_size("dp")
     total[...] = total_in_ref[...]
     for k in range(8):
-        add_product(total, theirs_ref, k * n, k % 2, weight_ref, residue_at(k // 2 + 1, 1 - core))
+        ref, at = (early_ref, late_ref)[k // 4], k % 4 * n
+        add_product(total, ref, at, k % 2, weight_ref, residue_at(k // 2 + 1, 1 - core))
     columns = total.shape[1]
     row = lax.broadcasted_iota(jnp.int32, (columns, columns), 0)
     col = lax.broadcasted_iota(jnp.int32, (columns, columns), 1)
@@ -134,7 +135,8 @@
     dp = lax.axis_size("dp")
     shape = jax.ShapeDtypeStruct
     other_weight = swapped(down_weight)
-    copies = lax.all_gather(tokens, "zo", axis=0)
+    copies = jnp.broadcast_to(tokens[None], (dp, rows, width))
+    copies = lax.all_to_all(copies, "zo", split_axis=0, concat_axis=0, tiled=True)
     copies = jnp.repeat(copies, 2, axis=0)
     pair = lax.all_to_all(copies, ("dp", "core"), split_axis=0, concat_axis=0, tiled=True)
     halves = (pair[:dp], pair[dp:])
@@ -146,7 +148,8 @@
     two = (first, second)
     four = tuple(shifted(a, 2, cores=(1,)) for a in two)
     three = shifted(jnp.concatenate(two), 1)
-    theirs = swapped(jnp.concatenate([one, *two, three, *four]))
+    early = swapped(jnp.concatenate([one, *two]))
+    late = swapped(jnp.concatenate([three, *four]))
     total = vmem_call(
         near_kernel,
         shape((dp * rows, columns), F32),
@@ -162,7 +165,8 @@
         up_kernel,
         (shape((dp * rows, columns), BF16), shape((rows, columns), BF16)),
         total,
-        theirs,
+        early,
+        late,
         gate_up_weight,
         flops=dp * rows * gate_up_weight.size,
         scratch=[pltpu.VMEM((dp * rows, columns), F32)],

time: 219 us -> 215 us (0.982)
  the two profiles are of different devices: /device:TPU:96 before, /device:TPU:104 now
where the time goes in v1:
time: 215 us; the launch traced here: 214 us
  starting transfers between devices  91.4 us (43%)
  blocking collectives  88.4 us (41%)
  waiting for transfers between devices  28.8 us (13%)
  Pallas kernels  3 us (1%)
    all_to_all x1, starting transfers between devices, per_device(): lax.all_to_all(copies, 'zo', split_axis=0, concat_axis=0, tiled=True)  42.1 us
    ppermute x10, starting transfers between devices, shifted(): return lax.ppermute(array, TENSOR, pairs)  37.3 us
    all_to_all x1, blocking collectives, per_device(): out = lax.all_to_all(out, 'zo', split_axis=0, concat_axis=0, tiled=True)  35.1 us
    all_to_all x1, waiting for transfers between devices, per_device(): lax.all_to_all(copies, 'zo', split_axis=0, concat_axis=0, tiled=True)  21.1 us
    all_to_all x1, blocking collectives, per_device(): parts = lax.all_to_all(parts, 'dp', split_axis=0, concat_axis=0, tiled=True)  12.9 us
    ppermute x3, starting transfers between devices, swapped(): return lax.ppermute(array, 'core', [(0, 1), (1, 0)])  12 us
    all_to_all x1, blocking collectives, per_device(): lax.all_to_all(copies, ('dp', 'core'), split_axis=0, concat_axis=0, tiled...  11.9 us
    all_to_all x1, blocking collectives, per_device(): lax.all_to_all(hidden, 'dp', split_axis=0, concat_axis=0, tiled=True)  9.1 us
  transfers between devices with their start and end apart: 14, of which 4 were waited for; matrix products, arithmetic and copies ran while one was open for 0% of the time, Pallas kernels for 0%

profile of v1, /device:TPU:104, one launch (start us, length us, event | category | flops | bytes accessed | tf_op | source)
XLA Modules:
  0.0 214.2 jit_solution(58490362060272569)
XLA Ops:
  0.0 1.4 broadcast_in_dim.6
  1.4 42.1 %all-to-all-start = ((bf16[4,128,128]{2,1,0:T(8,128)(2,1)}), bf16[4,128,128]{2,1,0:T(8,128)(2,1)S(1)}, u32[]{:S(2)}, u32[]{:S(2)}) async-start(bf16[4,128,128]{2,1,0:T(8,128)(2,1)} %broadcast_in_dim.6), calls=%async_computation | async-start | bytes 262144 | tf_op jit(solution)/shard_map/all_to_all | solution.py:139
  43.5 0.0 copy-start
  43.5 2.1 collective-permute-start.2
  45.6 21.1 %all-to-all-done = bf16[4,128,128]{2,1,0:T(8,128)(2,1)S(1)} async-done(((bf16[4,128,128]{2,1,0:T(8,128)(2,1)}), bf16[4,128,128]{2,1,0:T(8,128)(2,1)S(1)}, u32[]{:S(2)}, u32[]{:S(2)}) %all-to-all-start) | async-done | bytes 131104 | tf_op jit(solution)/shard_map/all_to_all | solution.py:139
  66.8 11.9 %all_to_all.30.refs_0_ = bf16[8,128,128]{2,1,0:T(8,128)(2,1)S(1)} all-to-all(bf16[8,128,128]{2,1,0:T(8,128)(2,1)S(1)} %bitcast.9), channel_id=1, replica_groups=mesh['groups'=2,'dp'=4,'zo'=4,'zi'=8,'core'=2] {'dp','core'}, dimensions={0} | all-to-all | bytes 524288 | tf_op jit(solution)/shard_map/all_to_all | solution.py:141
  78.7 5.2 %collective-permute-start.1 = (bf16[4,128,128]{2,1,0:T(8,128)(2,1)S(1)}, bf16[4,128,128]{2,1,0:T(8,128)(2,1)S(1)}, u32[]{:S(2)}, u32[]{:S(2)}) collective-permute-start(bf16[4,128,128]{2,1,0:T(8,128)(2,1)S(1)} %get-tuple-element.18), channel_id=1, source_target_pairs={{0,4},{1,61},{2,6},{3,63},{4,8},{5,1},{6,10},{7,3},{8,12},{9,5},{1... | collective-permute-start | bytes 393224 | tf_op jit(solution)/shard_map/ppermute | solution.py:21
  83.9 5.3 %collective-permute-start.3 = (bf16[4,128,128]{2,1,0:T(8,128)(2,1)S(1)}, bf16[4,128,128]{2,1,0:T(8,128)(2,1)S(1)}, u32[]{:S(2)}, u32[]{:S(2)}) collective-permute-start(bf16[4,128,128]{2,1,0:T(8,128)(2,1)S(1)} %get-tuple-element.20), channel_id=1, source_target_pairs={{0,4},{1,61},{2,6},{3,63},{4,8},{5,1},{6,10},{7,3},{8,12},{9,5},{1... | collective-permute-start | bytes 393224 | tf_op jit(solution)/shard_map/ppermute | solution.py:21
  89.2 7.7 %collective-permute-start = (bf16[8,128,128]{2,1,0:T(8,128)(2,1)S(1)}, bf16[8,128,128]{2,1,0:T(8,128)(2,1)S(1)}, u32[]{:S(2)}, u32[]{:S(2)}) collective-permute-start(bf16[8,128,128]{2,1,0:T(8,128)(2,1)S(1)} %all_to_all.30.refs_0_), channel_id=1, source_target_pairs={{0,2},{1,63},{2,4},{3,1},{4,6},{5,3},{6,8},{7,5},{8,10},{9,7},{10,... | collective-permute-start | bytes 786440 | tf_op jit(solution)/shard_map/ppermute | solution.py:21
  96.9 0.0 collective-permute-done.2.refs_2_
  96.9 0.0 collective-permute-done.1.refs_2_
  96.9 0.0 collective-permute-done.3.refs_3_
  97.0 3.6 %collective-permute-start.4 = (bf16[8,128,128]{2,1,0:T(8,128)(2,1)S(1)}, bf16[8,128,128]{2,1,0:T(8,128)(2,1)S(1)}, u32[]{:S(2)}, u32[]{:S(2)}) collective-permute-start(bf16[8,128,128]{2,1,0:T(8,128)(2,1)S(1)} %pad_maximum_fusion.2), channel_id=1, source_target_pairs={{0,2},{1,63},{2,4},{3,1},{4,6},{5,3},{6,8},{7,5},{8,10},{9,7},{10,... | collective-permute-start | bytes 786440 | tf_op jit(solution)/shard_map/ppermute | solution.py:21
  100.5 0.7 collective-permute-start.5
  101.2 0.7 collective-permute-start.6
  101.9 0.0 collective-permute-done.refs_1_
  101.9 0.1 pad_maximum_fusion
  102.0 4.8 %collective-permute-start.7 = (bf16[16,128,128]{2,1,0:T(8,128)(2,1)S(1)}, bf16[16,128,128]{2,1,0:T(8,128)(2,1)S(1)}, u32[]{:S(2)}, u32[]{:S(2)}) collective-permute-start(bf16[16,128,128]{2,1,0:T(8,128)(2,1)S(1)} %pad_maximum_fusion), channel_id=1, source_target_pairs={{0,1},{1,0},{2,3},{3,2},{4,5},{5,4},{6,7},{7,6},{8,9},{9,8},{10,11... | collective-permute-start | bytes 1572872 | tf_op jit(solution)/shard_map/ppermute | solution.py:34
  106.8 0.0 collective-permute-done.5.refs_5_
  106.8 0.0 collective-permute-done.6.refs_6_
  106.8 0.0 collective-permute-done.4.refs_4_
  106.8 0.1 pad_maximum_fusion.1
  106.9 5.1 %collective-permute-start.8 = (bf16[16,128,128]{2,1,0:T(8,128)(2,1)S(1)}, bf16[16,128,128]{2,1,0:T(8,128)(2,1)S(1)}, u32[]{:S(2)}, u32[]{:S(2)}) collective-permute-start(bf16[16,128,128]{2,1,0:T(8,128)(2,1)S(1)} %pad_maximum_fusion.1), channel_id=1, source_target_pairs={{0,1},{1,0},{2,3},{3,2},{4,5},{5,4},{6,7},{7,6},{8,9},{9,8},{10,11... | collective-permute-start | bytes 1572872 | tf_op jit(solution)/shard_map/ppermute | solution.py:34
  112.0 0.0 copy-done
  112.0 0.8 shard_map.37.refs_0_
  112.9 0.0 collective-permute-done.7.refs_1_
  112.9 0.6 collective-permute-done.8.refs_2_
  113.5 1.1 shard_map.38
  114.6 0.0 copy-start.1
  114.6 12.9 %all_to_all.31.refs_0_ = bf16[4,128,512]{2,1,0:T(8,128)(2,1)S(1)} all-to-all(bf16[4,128,512]{2,1,0:T(8,128)(2,1)S(1)} %bitcast.6), channel_id=1, replica_groups=mesh['groups'=2,'dp'=4,'zo'=4,'zi'=8,'core'=2] {'dp'}, dimensions={0} | all-to-all | bytes 1048576 | tf_op jit(solution)/shard_map/all_to_all | solution.py:175
  127.5 0.1 shard_map.39
  127.6 9.1 %all_to_all.32 = bf16[4,128,256]{2,1,0:T(8,128)(2,1)S(1)} all-to-all(bf16[4,128,256]{2,1,0:T(8,128)(2,1)S(1)} %broadcast_in_dim.8), channel_id=1, replica_groups=mesh['groups'=2,'dp'=4,'zo'=4,'zi'=8,'core'=2] {'dp'}, dimensions={0} | all-to-all | bytes 524288 | tf_op jit(solution)/shard_map/all_to_all | solution.py:180
  136.7 2.2 %all_gather.9.refs_0_ = bf16[2,512,256]{2,1,0:T(8,128)(2,1)S(1)} all-gather(bf16[1,512,256]{2,1,0:T(8,128)(2,1)S(1)} %bitcast.8), channel_id=1, replica_groups=mesh['groups'=2,'dp'=4,'zo'=4,'zi'=8,'core'=2] {'core'}, dimensions={0}, use_global_device_ids=true | all-gather | bytes 786432 | tf_op jit(solution)/shard_map/all_gather | solution.py:181
  138.9 0.0 copy-done.1
  138.9 0.9 shard_map.40
  139.8 2.0 collective-permute-start.10
  141.8 0.7 collective-permute-start.11
  142.5 5.7 %collective-permute-start.9 = (bf16[512,256]{1,0:T(8,128)(2,1)S(1)}, bf16[512,256]{1,0:T(8,128)(2,1)S(1)}, u32[]{:S(2)}, u32[]{:S(2)}) collective-permute-start(bf16[512,256]{1,0:T(8,128)(2,1)S(1)} %get-tuple-element.25), channel_id=1, source_target_pairs={{0,62},{1,3},{2,0},{3,5},{4,2},{5,7},{6,4},{7,9},{8,6},{9,11},{10,... | collective-permute-start | bytes 786440 | tf_op jit(solution)/shard_map/ppermute | solution.py:21
  148.2 0.5 collective-permute-done.10
  148.7 0.0 collective-permute-done.11
  148.7 0.1 add_convert_fusion
  148.8 5.8 %collective-permute-start.12 = (bf16[512,256]{1,0:T(8,128)(2,1)S(1)}, bf16[512,256]{1,0:T(8,128)(2,1)S(1)}, u32[]{:S(2)}, u32[]{:S(2)}) collective-permute-start(bf16[512,256]{1,0:T(8,128)(2,1)S(1)} %add_convert_fusion), channel_id=1, source_target_pairs={{0,60},{1,5},{2,62},{3,7},{4,0},{5,9},{6,2},{7,11},{8,4},{9,13},{1... | collective-permute-start | bytes 786440 | tf_op jit(solution)/shard_map/ppermute | solution.py:21
  154.6 0.0 collective-permute-done.9.refs_0_.refs_1_
  154.6 6.6 %collective-permute-done.12.refs_1_.refs_2_ = bf16[512,256]{1,0:T(8,128)(2,1)S(1)} collective-permute-done((bf16[512,256]{1,0:T(8,128)(2,1)S(1)}, bf16[512,256]{1,0:T(8,128)(2,1)S(1)}, u32[]{:S(2)}, u32[]{:S(2)}) %collective-permute-start.12) | collective-permute-done | bytes 262176 | tf_op jit(solution)/shard_map/ppermute | solution.py:21
  161.2 8.8 %all-gather = f32[1024,128]{1,0:T(8,128)S(1)} all-gather(f32[512,128]{1,0:T(8,128)S(1)} %shard_map.41), channel_id=2, replica_groups=mesh['groups'=2,'dp'=4,'zo'=4,'zi'=8,'core'=2] {'core'}, dimensions={0}, use_global_device_ids=true | all-gather | bytes 786432 | tf_op jit(solution)/shard_map/all_gather | solution.py:197
  170.0 0.1 shard_map.42
  170.0 8.5 %all_to_all.33 = bf16[4,128,128]{2,1,0:T(8,128)(2,1)S(1)} all-to-all(bf16[4,128,128]{2,1,0:T(8,128)(2,1)S(1)} %bitcast.7), channel_id=1, replica_groups=mesh['groups'=2,'dp'=4,'zo'=4,'zi'=8,'core'=2] {'dp'}, dimensions={0} | all-to-all | bytes 262144 | tf_op jit(solution)/shard_map/all_to_all | solution.py:200
  178.5 35.1 %all_to_all.34 = bf16[4,128,128]{2,1,0:T(8,128)(2,1)S(1)} all-to-all(bf16[4,128,128]{2,1,0:T(8,128)(2,1)S(1)} %all_to_all.33), channel_id=1, replica_groups=mesh['groups'=2,'dp'=4,'zo'=4,'zi'=8,'core'=2] {'zo'}, dimensions={0} | all-to-all | bytes 262144 | tf_op jit(solution)/shard_map/all_to_all | solution.py:201
  213.6 0.6 reduce_sum.12
  (5 shorter events, 0.1 us)
Async XLA Ops:
  1.4 65.3 %all-to-all-start = ((bf16[4,128,128]{2,1,0:T(8,128)(2,1)}), bf16[4,128,128]{2,1,0:T(8,128)(2,1)S(1)}, u32[]{:S(2)}, u32[]{:S(2)}) async-start(bf16[4,128,128]{2,1,0:T(8,128)(2,1)} %broadcast_in_dim.6), calls=%async_computation | async-start | bytes 262144 | tf_op jit(solution)/shard_map/all_to_all | solution.py:139
  43.5 68.5 %copy-start = (bf16[2048,512]{1,0:T(8,128)(2,1)S(1)}, bf16[2048,512]{1,0:T(8,128)(2,1)}, u32[]{:S(2)}) copy-start(bf16[2048,512]{1,0:T(8,128)(2,1)} %refs_3_.1) | copy-start | bytes 6291460
  43.5 53.4 %collective-permute-start.2 = (bf16[256,2048]{1,0:T(8,128)(2,1)}, bf16[256,2048]{1,0:T(8,128)(2,1)S(1)}, u32[]{:S(2)}, u32[]{:S(2)}) collective-permute-start(bf16[256,2048]{1,0:T(8,128)(2,1)} %refs_1_.1), channel_id=1, source_target_pairs={{0,1},{1,0},{2,3},{3,2},{4,5},{5,4},{6,7},{7,6},{8,9},{9,8},{10,11... | collective-permute-start | bytes 3145736 | tf_op jit(solution)/shard_map/ppermute | solution.py:34
  78.7 18.2 %collective-permute-start.1 = (bf16[4,128,128]{2,1,0:T(8,128)(2,1)S(1)}, bf16[4,128,128]{2,1,0:T(8,128)(2,1)S(1)}, u32[]{:S(2)}, u32[]{:S(2)}) collective-permute-start(bf16[4,128,128]{2,1,0:T(8,128)(2,1)S(1)} %get-tuple-element.18), channel_id=1, source_target_pairs={{0,4},{1,61},{2,6},{3,63},{4,8},{5,1},{6,10},{7,3},{8,12},{9,5},{1... | collective-permute-start | bytes 393224 | tf_op jit(solution)/shard_map/ppermute | solution.py:21
  83.9 13.0 %collective-permute-start.3 = (bf16[4,128,128]{2,1,0:T(8,128)(2,1)S(1)}, bf16[4,128,128]{2,1,0:T(8,128)(2,1)S(1)}, u32[]{:S(2)}, u32[]{:S(2)}) collective-permute-start(bf16[4,128,128]{2,1,0:T(8,128)(2,1)S(1)} %get-tuple-element.20), channel_id=1, source_target_pairs={{0,4},{1,61},{2,6},{3,63},{4,8},{5,1},{6,10},{7,3},{8,12},{9,5},{1... | collective-permute-start | bytes 393224 | tf_op jit(solution)/shard_map/ppermute | solution.py:21
  89.2 12.7 %collective-permute-start = (bf16[8,128,128]{2,1,0:T(8,128)(2,1)S(1)}, bf16[8,128,128]{2,1,0:T(8,128)(2,1)S(1)}, u32[]{:S(2)}, u32[]{:S(2)}) collective-permute-start(bf16[8,128,128]{2,1,0:T(8,128)(2,1)S(1)} %all_to_all.30.refs_0_), channel_id=1, source_target_pairs={{0,2},{1,63},{2,4},{3,1},{4,6},{5,3},{6,8},{7,5},{8,10},{9,7},{10,... | collective-permute-start | bytes 786440 | tf_op jit(solution)/shard_map/ppermute | solution.py:21
  97.0 9.8 %collective-permute-start.4 = (bf16[8,128,128]{2,1,0:T(8,128)(2,1)S(1)}, bf16[8,128,128]{2,1,0:T(8,128)(2,1)S(1)}, u32[]{:S(2)}, u32[]{:S(2)}) collective-permute-start(bf16[8,128,128]{2,1,0:T(8,128)(2,1)S(1)} %pad_maximum_fusion.2), channel_id=1, source_target_pairs={{0,2},{1,63},{2,4},{3,1},{4,6},{5,3},{6,8},{7,5},{8,10},{9,7},{10,... | collective-permute-start | bytes 786440 | tf_op jit(solution)/shard_map/ppermute | solution.py:21
  100.5 6.2 %collective-permute-start.5 = (bf16[4,128,128]{2,1,0:T(8,128)(2,1)S(1)}, bf16[4,128,128]{2,1,0:T(8,128)(2,1)S(1)}, u32[]{:S(2)}, u32[]{:S(2)}) collective-permute-start(bf16[4,128,128]{2,1,0:T(8,128)(2,1)S(1)} %collective-permute-done.1.refs_2_), channel_id=1, source_target_pairs={{1,61},{3,63},{5,1},{7,3},{9,5},{11,7},{13,9},{15,11},{17,13},{19,... | collective-permute-start | bytes 393224 | tf_op jit(solution)/shard_map/ppermute | solution.py:21
  101.2 5.6 %collective-permute-start.6 = (bf16[4,128,128]{2,1,0:T(8,128)(2,1)S(1)}, bf16[4,128,128]{2,1,0:T(8,128)(2,1)S(1)}, u32[]{:S(2)}, u32[]{:S(2)}) collective-permute-start(bf16[4,128,128]{2,1,0:T(8,128)(2,1)S(1)} %collective-permute-done.3.refs_3_), channel_id=1, source_target_pairs={{1,61},{3,63},{5,1},{7,3},{9,5},{11,7},{13,9},{15,11},{17,13},{19,... | collective-permute-start | bytes 393224 | tf_op jit(solution)/shard_map/ppermute | solution.py:21
  102.0 10.9 %collective-permute-start.7 = (bf16[16,128,128]{2,1,0:T(8,128)(2,1)S(1)}, bf16[16,128,128]{2,1,0:T(8,128)(2,1)S(1)}, u32[]{:S(2)}, u32[]{:S(2)}) collective-permute-start(bf16[16,128,128]{2,1,0:T(8,128)(2,1)S(1)} %pad_maximum_fusion), channel_id=1, source_target_pairs={{0,1},{1,0},{2,3},{3,2},{4,5},{5,4},{6,7},{7,6},{8,9},{9,8},{10,11... | collective-permute-start | bytes 1572872 | tf_op jit(solution)/shard_map/ppermute | solution.py:34
  106.9 6.6 %collective-permute-start.8 = (bf16[16,128,128]{2,1,0:T(8,128)(2,1)S(1)}, bf16[16,128,128]{2,1,0:T(8,128)(2,1)S(1)}, u32[]{:S(2)}, u32[]{:S(2)}) collective-permute-start(bf16[16,128,128]{2,1,0:T(8,128)(2,1)S(1)} %pad_maximum_fusion.1), channel_id=1, source_target_pairs={{0,1},{1,0},{2,3},{3,2},{4,5},{5,4},{6,7},{7,6},{8,9},{9,8},{10,11... | collective-permute-start | bytes 1572872 | tf_op jit(solution)/shard_map/ppermute | solution.py:34
  114.6 24.3 %copy-start.1 = (bf16[256,2048]{1,0:T(8,128)(2,1)S(1)}, bf16[256,2048]{1,0:T(8,128)(2,1)}, u32[]{:S(2)}) copy-start(bf16[256,2048]{1,0:T(8,128)(2,1)} %refs_1_.1) | copy-start | bytes 3145732
  139.8 8.9 %collective-permute-start.10 = (bf16[512,256]{1,0:T(8,128)(2,1)S(1)}, bf16[512,256]{1,0:T(8,128)(2,1)S(1)}, u32[]{:S(2)}, u32[]{:S(2)}) collective-permute-start(bf16[512,256]{1,0:T(8,128)(2,1)S(1)} %get-tuple-element.27), channel_id=1, source_target_pairs={{0,62},{1,3},{2,0},{3,5},{4,2},{5,7},{6,4},{7,9},{8,6},{9,11},{10,... | collective-permute-start | bytes 786440 | tf_op jit(solution)/shard_map/ppermute | solution.py:21
  141.8 6.9 %collective-permute-start.11 = (bf16[512,256]{1,0:T(8,128)(2,1)S(1)}, bf16[512,256]{1,0:T(8,128)(2,1)S(1)}, u32[]{:S(2)}, u32[]{:S(2)}) collective-permute-start(bf16[512,256]{1,0:T(8,128)(2,1)S(1)} %get-tuple-element.28), channel_id=1, source_target_pairs={{1,5},{3,7},{5,9},{7,11},{9,13},{11,15},{13,17},{15,19},{17,21},{1... | collective-permute-start | bytes 786440 | tf_op jit(solution)/shard_map/ppermute | solution.py:21
  142.5 12.1 %collective-permute-start.9 = (bf16[512,256]{1,0:T(8,128)(2,1)S(1)}, bf16[512,256]{1,0:T(8,128)(2,1)S(1)}, u32[]{:S(2)}, u32[]{:S(2)}) collective-permute-start(bf16[512,256]{1,0:T(8,128)(2,1)S(1)} %get-tuple-element.25), channel_id=1, source_target_pairs={{0,62},{1,3},{2,0},{3,5},{4,2},{5,7},{6,4},{7,9},{8,6},{9,11},{10,... | collective-permute-start | bytes 786440 | tf_op jit(solution)/shard_map/ppermute | solution.py:21
  148.8 12.4 %collective-permute-start.12 = (bf16[512,256]{1,0:T(8,128)(2,1)S(1)}, bf16[512,256]{1,0:T(8,128)(2,1)S(1)}, u32[]{:S(2)}, u32[]{:S(2)}) collective-permute-start(bf16[512,256]{1,0:T(8,128)(2,1)S(1)} %add_convert_fusion), channel_id=1, source_target_pairs={{0,60},{1,5},{2,62},{3,7},{4,0},{5,9},{6,2},{7,11},{8,4},{9,13},{1... | collective-permute-start | bytes 786440 | tf_op jit(solution)/shard_map/ppermute | solution.py:21
